TPU v7x, 32 devices: a whole 2x2x4 slice. The times are simulated.
32 devices in a mesh: sta: 16 (over z, x, core), tpl: 2 (over y).
Axes of the slice: x: 2, y: 2, z: 4, core: 2. Of those that a mesh axis runs over, the one named last changes fastest.
Arguments:
- waveform: bfloat16 [16, 3, 4279], P('sta'), may hold values from -150 to 150
- templates: bfloat16 [128, 16, 1536], P('tpl', 'sta'), may hold values from -6 to 6
- lags: int32 [128, 16], P('tpl', 'sta'), may hold values from 0 to 3000
- present: int32 [128, 16], P('tpl', 'sta'), may hold values 0 or 1
Outputs:
- score: float32 [768, 128], P('sta', 'tpl')
- scale_mad: float32 [128], P('tpl')
- peak: float32 [768], P('sta')
All inputs are finite; a program needn't handle non-finite values. No bound on the sum of `present` on one device may be relied on, other than what follows from the above.
Results may differ from a plain program's by a relative error of at most 0.0003.
Values may be sent and summed in bfloat16 or wider, within the bound.
A program may use at most 64 MiB of HBM per device.

v0:
```python
import jax
import jax.numpy as jnp
from jax import lax
from jax.sharding import PartitionSpec as P

LEN = 512
LAG = 3000
BINS = 1024
TOUT_DEV = 48


def toeplitz_rows(record, length, columns):
    count = record.shape[1]
    chans = record.shape[0]
    tiled = jnp.broadcast_to(record[:, None, :], (chans, length + 1, count))
    tiled = tiled.reshape(chans, (length + 1) * count)[:, : length * (count + 1)]
    tiled = tiled.reshape(chans, length, count + 1)[:, :, :columns]
    return tiled.reshape(chans * length, columns)


def shift_rows(block, offsets, count):
    return jax.vmap(lambda row, offset: lax.dynamic_slice_in_dim(row, offset, count))(
        block, offsets
    )


def hat_counts(values, nbins):
    width = 512.0 / nbins
    ncols = values.shape[1]
    position = jnp.clip(jnp.abs(values) / width - 0.5, 0.0, nbins - 1.0)
    lower = jnp.minimum(jnp.floor(position), nbins - 2.0)
    weight = position - lower
    index = lower.astype(jnp.int32) + nbins * jnp.arange(ncols, dtype=jnp.int32)[None, :]
    flat_index = index.reshape(-1)
    flat_weight = weight.reshape(-1)
    counts = jax.ops.segment_sum(1.0 - flat_weight, flat_index, num_segments=ncols * nbins)
    counts = counts + jax.ops.segment_sum(flat_weight, flat_index + 1, num_segments=ncols * nbins)
    return counts.reshape(ncols, nbins)


def median_abs(counts, halfway):
    width = 512.0 / counts.shape[1]
    running = jnp.cumsum(counts, axis=1)
    earlier = running - counts
    share = jnp.clip((halfway - earlier) / jnp.maximum(counts, 1.0), 0.0, 1.0)
    return width * jnp.sum(share, axis=1)


def correlate_record(record, pattern, scaling, span):
    block_rows = 1024
    blocks = -(-span // block_rows)
    padded = jnp.pad(record, ((0, 0), (0, blocks * block_rows + LEN - record.shape[1])))

    def correlate(number, corr):
        begin = number * block_rows
        segment = lax.dynamic_slice_in_dim(padded, begin, block_rows + LEN, 1)
        columns = toeplitz_rows(segment, LEN, block_rows)
        result = jnp.dot(pattern, columns, preferred_element_type=jnp.float32) / scaling[:, None]
        return lax.dynamic_update_slice_in_dim(corr, result, begin, 1)

    return lax.fori_loop(
        0, blocks, correlate, jnp.zeros((pattern.shape[0], blocks * block_rows), jnp.float32)
    )


def on_device(waveform, templates, lags, present):
    stations = lax.axis_size("sta")
    total = TOUT_DEV * stations
    span = total + LAG
    record = waveform[0]
    pattern = templates[:, 0, :]
    offsets = lags[:, 0]
    member = present[:, 0].astype(jnp.float32)
    scaling = jnp.sqrt(jnp.sum(pattern.astype(jnp.float32) ** 2, axis=1) + 1e-06)
    corr = correlate_record(record, pattern, scaling, span)
    moved = shift_rows(corr, offsets, total) * member[:, None]
    arrived = lax.all_to_all(moved, "sta", split_axis=1, concat_axis=0, tiled=True)
    owned = jnp.sum(arrived.reshape(stations, moved.shape[0], TOUT_DEV), axis=0)
    stack = owned.T
    counts = hat_counts(stack, BINS)
    summed = lax.psum(counts, "sta")
    median = median_abs(summed, 0.5 * total)
    scale_mad = 1.4826 * median
    score = stack / scale_mad[None, :]
    local_best = jnp.max(score, axis=1)
    peak = lax.pmax(local_best, "tpl")
    return (score, scale_mad, peak)


def solution(mesh):
    placed = (P("sta", None, None), P("tpl", "sta", None), P("tpl", "sta"), P("tpl", "sta"))
    return jax.shard_map(
        on_device,
        mesh=mesh,
        in_specs=placed,
        out_specs=(P("sta", "tpl"), P("tpl"), P("sta")),
        check_vma=False,
    )
```

profile of v0, /device:TPU:0, one launch (start us, length us, event | category | flops | bytes accessed | tf_op | source)
XLA Modules:
  0.0 590.2 jit_solution(13781624587618451553)
XLA Ops:
  10.1 143.2 %while.14 = (s32[]{:T(128)}, f32[64,4096]{1,0:T(8,128)}, bf16[3,4608]{1,0:T(4,128)(2,1)S(1)}, bf16[64,1536]{1,0:T(8,128)(2,1)}, f32[64]{0:T(128)S(1)}, /*index=5...) while((s32[]{:T(128)}, f32[64,4096]{1,0:T(8,128)}, bf16[3,4608]{1,0:T(4,128)(2,1)S(1)}, ...), condition=%wide.region_2.3_spmd, body=%wide.region_1.2_spmd.sunk | while | flops 201392128 | bytes 56369640 | solution.py:61
  10.1 2.5 broadcast_bitcast_fusion.2
  12.6 5.6 copy.35
  18.2 3.9 slice.42
  22.1 9.1 %reshape.114 = bf16[2360832]{0:T(1024)(128)(2,1)} reshape(bf16[3,786944]{1,0:T(4,128)(2,1)} %slice.42) | data formatting | bytes 9443328 | tf_op jit(solution)/shard_map/while
  31.2 11.4 %reshape.115 = bf16[3,512,1537]{2,1,0:T(8,128)(2,1)} reshape(bf16[2360832]{0:T(1024)(128)(2,1)} %reshape.114) | data formatting | bytes 9443328 | tf_op jit(solution)/shard_map/while/body/eval_jaxpr/reshape | solution.py:17
  45.9 2.5 broadcast_bitcast_fusion.2
  48.4 5.6 copy.35
  54.0 3.9 slice.42
  57.9 9.1 %reshape.114 = bf16[2360832]{0:T(1024)(128)(2,1)} reshape(bf16[3,786944]{1,0:T(4,128)(2,1)} %slice.42) | data formatting | bytes 9443328 | tf_op jit(solution)/shard_map/while
  67.0 11.4 %reshape.115 = bf16[3,512,1537]{2,1,0:T(8,128)(2,1)} reshape(bf16[2360832]{0:T(1024)(128)(2,1)} %reshape.114) | data formatting | bytes 9443328 | tf_op jit(solution)/shard_map/while/body/eval_jaxpr/reshape | solution.py:17
  81.7 2.5 broadcast_bitcast_fusion.2
  84.2 5.6 copy.35
  89.8 3.9 slice.42
  93.7 9.1 %reshape.114 = bf16[2360832]{0:T(1024)(128)(2,1)} reshape(bf16[3,786944]{1,0:T(4,128)(2,1)} %slice.42) | data formatting | bytes 9443328 | tf_op jit(solution)/shard_map/while
  102.8 11.4 %reshape.115 = bf16[3,512,1537]{2,1,0:T(8,128)(2,1)} reshape(bf16[2360832]{0:T(1024)(128)(2,1)} %reshape.114) | data formatting | bytes 9443328 | tf_op jit(solution)/shard_map/while/body/eval_jaxpr/reshape | solution.py:17
  117.5 2.5 broadcast_bitcast_fusion.2
  120.0 5.6 copy.35
  125.6 3.9 slice.42
  129.5 9.1 %reshape.114 = bf16[2360832]{0:T(1024)(128)(2,1)} reshape(bf16[3,786944]{1,0:T(4,128)(2,1)} %slice.42) | data formatting | bytes 9443328 | tf_op jit(solution)/shard_map/while
  138.6 11.4 %reshape.115 = bf16[3,512,1537]{2,1,0:T(8,128)(2,1)} reshape(bf16[2360832]{0:T(1024)(128)(2,1)} %reshape.114) | data formatting | bytes 9443328 | tf_op jit(solution)/shard_map/while/body/eval_jaxpr/reshape | solution.py:17
  153.3 260.9 %while.15 = (s32[]{:T(128)}, f32[64,4096]{1,0:T(8,128)}, s32[64,2]{0,1:T(2,128)S(1)}, f32[64,768]{1,0:T(8,128)}, s32[]{:T(128)}, /*index=5*/s32[]{:T(128)}) while((s32[]{:T(128)}, f32[64,4096]{1,0:T(8,128)}, s32[64,2]{0,1:T(2,128)S(1)}, f32[64,768]{1,0:T(8,128)}, s32[]{:T(128)}, /*index=5*/s32[]{:T(128)}) %tuple.53), condition=%wide.while_cond, body=%wide.while_body.sunk | while | flops 2 | bytes 12401 | solution.py:22
  153.9 2.1 dynamic-slice.7
  158.0 2.1 dynamic-slice.7
  170.2 2.1 dynamic-slice.7
  174.3 2.1 dynamic-slice.7
  178.3 2.1 dynamic-slice.7
  190.5 2.1 dynamic-slice.7
  194.6 2.1 dynamic-slice.7
  198.7 2.1 dynamic-slice.7
  202.8 2.1 dynamic-slice.7
  211.0 2.1 dynamic-slice.7
  219.1 2.1 dynamic-slice.7
  223.2 2.1 dynamic-slice.7
  227.3 2.1 dynamic-slice.7
  231.4 2.1 dynamic-slice.7
  235.5 2.1 dynamic-slice.7
  239.5 2.1 dynamic-slice.7
  243.6 2.1 dynamic-slice.7
  247.7 2.1 dynamic-slice.7
  255.9 2.1 dynamic-slice.7
  259.9 2.1 dynamic-slice.7
  416.8 7.4 %all-to-all-start = ((f32[16,1,3072]{2,1,0:T(1,128)}), f32[16,1,3072]{2,1,0:T(1,128)S(1)}, u32[]{:S(2)}, u32[]{:S(2)}) async-start(f32[16,1,3072]{2,1,0:T(1,128)} %reshape.110), calls=%async_computation | async-start | bytes 393216 | tf_op jit(solution)/shard_map/all_to_all | solution.py:77
  424.2 8.9 %all-to-all-done = f32[16,1,3072]{2,1,0:T(1,128)S(1)} async-done(((f32[16,1,3072]{2,1,0:T(1,128)}), f32[16,1,3072]{2,1,0:T(1,128)S(1)}, u32[]{:S(2)}, u32[]{:S(2)}) %all-to-all-start) | async-done | bytes 196640 | tf_op jit(solution)/shard_map/all_to_all | solution.py:77
  435.1 32.6 %scatter_custom_fusion = f32[65536]{0:T(1024)S(1)} fusion(s32[6144]{0:T(1024)S(1)} %bitcast.72, f32[6144]{0:T(1024)S(1)} %pad_maximum_fusion, f32[]{:T(128)} %constant.61.clone.1), kind=kCustom, calls=%fused_computation.15 | custom fusion | flops 6144 | bytes 262148 | tf_op jit(solution)/shard_map/add | solution.py:37
  468.6 87.8 %all-reduce.3.cloned.1.call-done = f32[64,1024]{1,0:T(8,128)} async-done(((f32[64,1024]{1,0:T(8,128)}), f32[64,1024]{1,0:T(8,128)}) %all-reduce.3.cloned.1.call-update) | async-done | bytes 262160 | tf_op jit(solution)/shard_map/psum | solution.py:81
  557.4 18.0 %reduce-window.6 = f32[64,8,128]{2,1,0:T(8,128)S(1)} reduce-window(f32[64,8,128]{2,1,0:T(8,128)S(1)} %bitcast.70, f32[]{:T(128)} %constant.61.clone.1), window={size=1x1x128 pad=0_0x0_0x127_0}, to_apply=%region_6.7 | reduce-window | flops 8323072 | bytes 524292 | tf_op jit(solution)/shard_map/reduce-window
  577.9 5.4 pmax.7
  (307 shorter events, 243.5 us)
Async XLA Ops:
  10.1 143.2 %copy-start.2 = (s32[64,1]{0,1:T(1,128)S(1)}, s32[64,1]{0,1:T(1,128)}, u32[]{:S(2)}) copy-start(s32[64,1]{0,1:T(1,128)} %param.8) | copy-start | bytes 772
  10.1 405.3 %copy-start.3 = (s32[64,1]{0,1:T(1,128)S(1)}, s32[64,1]{0,1:T(1,128)}, u32[]{:S(2)}) copy-start(s32[64,1]{0,1:T(1,128)} %param.9) | copy-start | bytes 772
  42.6 2.0 slice-start
  42.6 2.0 copy-start
  78.4 2.0 slice-start
  78.4 2.0 copy-start
  114.1 2.0 slice-start
  114.2 2.0 copy-start
  149.9 2.0 slice-start
  149.9 2.0 copy-start
  416.8 16.4 %all-to-all-start = ((f32[16,1,3072]{2,1,0:T(1,128)}), f32[16,1,3072]{2,1,0:T(1,128)S(1)}, u32[]{:S(2)}, u32[]{:S(2)}) async-start(f32[16,1,3072]{2,1,0:T(1,128)} %reshape.110), calls=%async_computation | async-start | bytes 393216 | tf_op jit(solution)/shard_map/all_to_all | solution.py:77
  424.2 132.2 %all-reduce.3.cloned.1.call-start = ((), (), s32[]{:S(2)}) async-start(), calls=%async_computation.1 | async-start | bytes 524288 | tf_op jit(solution)/shard_map/psum | solution.py:81
  577.1 6.2 %copy-start.1 = (f32[64]{0:T(128)}, f32[64]{0:T(128)S(1)}, u32[]{:S(2)}) copy-start(f32[64]{0:T(128)S(1)} %broadcast_multiply_fusion.1) | copy-start | bytes 772
Sparse Core Ops, SparseCore 0:
  468.7 87.6 all-reduce.2
where the time goes:
time: 600 us; the launch traced here: 590 us
  local copies, waits for them, and re-layouts  406 us (68%)
  waiting for transfers between devices  96.7 us (16%)
  other arithmetic  54.5 us (9%)
  between operations  14.2 us (2%)
  starting transfers between devices  7.43 us (1%)
    gather x256, local copies, waits for them, and re-layouts  261 us
    psum x1, waiting for transfers between devices, on_device(): summed = lax.psum(counts, 'sta')  87.8 us
    while x20, local copies, waits for them, and re-layouts  68.7 us
    reshape x4, local copies, waits for them, and re-layouts, toeplitz_rows(): tiled = tiled.reshape(chans, length, count + 1)[:, :, :columns]  45.5 us
    add x1, other arithmetic, hat_counts(): counts + jax.ops.segment_sum(flat_weight, flat_index + 1, num_segments=nc...  32.6 us
    another operation x4, other arithmetic  18.2 us
    slice x4, local copies, waits for them, and re-layouts, toeplitz_rows(): tiled = tiled.reshape(chans, (length + 1) * count)[:, :length * (count + 1)]  15.5 us
  transfers between devices with their start and end apart: 2, of which 2 were waited for; matrix products, arithmetic and copies ran while one was open for 0% of the time, Pallas kernels for 0%

commit v1 on v0

v1 whole, which is shorter than its diff:
```python
import functools

import jax
import jax.numpy as jnp
from jax import lax
from jax.experimental import pallas as pl
from jax.experimental.pallas import tpu as pltpu
from jax.sharding import PartitionSpec as P

LEN = 512
LAG = 3000
BINS = 1024
TOUT_DEV = 48
LANES = 128
MESH = pl.DeviceIdType.MESH


def ceil_to(value, step):
    return -(-value // step) * step


def correlate_kernel(blocks, stride, lags_ref, wave_ref, pattern_ref, present_ref, moved_ref, record, hankel, corr):
    chans, samples = wave_ref.shape
    rows = pattern_ref.shape[0]
    padded = record.shape[1]
    span = hankel.shape[2]
    width = padded - LANES
    record[...] = jnp.zeros_like(record)
    record[:, :samples] = wave_ref[...].astype(jnp.float32)
    row = lax.broadcasted_iota(jnp.int32, (8, padded), 0)
    for c in range(chans):
        base = jnp.broadcast_to(record[c : c + 1, :], (8, padded))
        for bit in (1, 2, 4):
            base = jnp.where((row & bit) != 0, pltpu.roll(base, padded - bit, 1), base)
        for g in range(LANES // 16):
            low = pltpu.roll(base, padded - 16 * g, 1) if g else base
            high = pltpu.roll(base, padded - 16 * g - 8, 1)
            both = jnp.concatenate([low[:, :span], high[:, :span]], axis=0)
            hankel[c, 16 * g : 16 * g + 16, :] = both.astype(jnp.bfloat16)
    pattern = pattern_ref[...]
    wide = pattern.astype(jnp.float32)
    scaling = jnp.sqrt(jnp.sum(wide * wide, axis=1, keepdims=True) + 1e-06)
    factor = present_ref[...].astype(jnp.float32) / scaling
    for b in range(blocks):
        parts = []
        for c in range(chans):
            for q in range(LEN // LANES):
                begin = 2 * LANES * b + LANES * q
                parts.append(hankel[c, :, begin : begin + 2 * LANES])
        columns = jnp.concatenate(parts, axis=0)
        result = jnp.dot(pattern, columns, preferred_element_type=jnp.float32) * factor
        corr[pl.ds(2 * b, rows, stride=stride), :] = result[:, :LANES]
        corr[pl.ds(2 * b + 1, rows, stride=stride), :] = result[:, LANES:]
    count = moved_ref.shape[0] // rows
    lane = lax.broadcasted_iota(jnp.int32, (count, LANES), 1)
    for t in range(rows):
        lag = lags_ref[t]
        begin = t * stride + (lag >> 7)
        rest = lag & (LANES - 1)
        near = corr[pl.ds(begin, count), :]
        after = corr[pl.ds(begin + 1, count), :]
        joined = jnp.where(lane >= rest, near, after)
        moved_ref[t * count : (t + 1) * count, :] = pltpu.roll(joined, (LANES - rest) & (LANES - 1), 1)


def correlate(wave, pattern, lags, present, total):
    chans, samples = wave.shape
    rows = pattern.shape[0]
    blocks = -(-(total + LAG) // (2 * LANES))
    span = 2 * LANES * blocks + LEN - LANES
    padded = span + LANES
    count = total // LANES
    stride = max(2 * blocks, LAG // LANES + count + 2) | 1
    return pl.pallas_call(
        functools.partial(correlate_kernel, blocks, stride),
        out_shape=jax.ShapeDtypeStruct((rows * count, LANES), jnp.float32),
        in_specs=[pl.BlockSpec(memory_space=pltpu.SMEM)] + [pl.BlockSpec(memory_space=pltpu.VMEM)] * 3,
        out_specs=pl.BlockSpec(memory_space=pltpu.VMEM),
        scratch_shapes=[
            pltpu.VMEM((chans, padded), jnp.float32),
            pltpu.VMEM((chans, LANES, span), jnp.bfloat16),
            pltpu.VMEM((rows * stride, LANES), jnp.float32),
        ],
    )(lags, wave, pattern, present)


def deviation_scale(stack, groups, total):
    width = 512.0 / BINS
    count = stack.shape[0] // groups
    position = jnp.clip(jnp.abs(stack) / width - 0.5, 0.0, BINS - 1.0)
    lower = jnp.minimum(jnp.floor(position), BINS - 2.0)
    coarse = jnp.floor(lower * 0.125)
    fine = position - 8.0 * coarse
    sub = lax.broadcasted_iota(jnp.int32, (LANES, LANES), 0).astype(jnp.float32)
    few = lax.broadcasted_iota(jnp.int32, (16, LANES), 0).astype(jnp.float32)
    tables = []
    for t in range(groups):
        hots, weights = [], []
        for a in range(count):
            r = t * count + a
            hots.append((coarse[r : r + 1, :] == sub).astype(jnp.float32).astype(jnp.bfloat16))
            hat = jnp.maximum(1.0 - jnp.abs(fine[r : r + 1, :] - few), 0.0)
            first = hat.astype(jnp.bfloat16)
            left = hat - first.astype(jnp.float32)
            second = left.astype(jnp.bfloat16)
            third = (left - second.astype(jnp.float32)).astype(jnp.bfloat16)
            weights.append(jnp.concatenate([first, second, third], axis=0))
        hot = jnp.concatenate(hots, axis=1)
        weight = jnp.concatenate(weights, axis=1)
        found = lax.dot_general(weight, hot, (((1,), (1,)), ((), ())), preferred_element_type=jnp.float32)
        found = found[:16] + found[16:32] + found[32:48]
        tables.append(found[:8] + pltpu.roll(found[8:], 1, 1))
    counts = jnp.concatenate(tables, axis=0)
    row = lax.broadcasted_iota(jnp.int32, counts.shape, 0) & 7
    running = counts
    for step in (1, 2, 4):
        running = running + jnp.where(row >= step, pltpu.roll(running, step, 0), 0.0)
    sums = [jnp.broadcast_to(jnp.sum(t, axis=0, keepdims=True), (8, LANES)) for t in tables]
    sums = jnp.concatenate(sums, axis=0)
    upper = (
        lax.broadcasted_iota(jnp.int32, (LANES, LANES), 0) < lax.broadcasted_iota(jnp.int32, (LANES, LANES), 1)
    ).astype(jnp.float32)
    prior = jnp.dot(sums, upper, precision=lax.Precision.HIGHEST, preferred_element_type=jnp.float32)
    earlier = prior + (running - counts)
    share = jnp.clip((0.5 * total - earlier) / jnp.maximum(counts, 1.0), 0.0, 1.0)
    scales = []
    for t in range(groups):
        part = jnp.sum(share[8 * t : 8 * t + 8], axis=0, keepdims=True)
        scales.append(1.4826 * (width * jnp.sum(part, axis=1, keepdims=True)))
    return scales


def exchange_kernel(n, m, moved_ref, score_ref, scale_ref, peak_ref, recv1, scored, send2, recv2, grid, best, bests, send1_sem, recv1_sem, send2_sem, recv2_sem, send3_sem, recv3_sem):
    me, group = lax.axis_index("sta"), lax.axis_index("tpl")
    groups = send2.shape[1]
    chunk = moved_ref.shape[0] // n
    count = chunk // groups
    own = score_ref.shape[0]

    def peer(d):
        return lax.rem(me + d, n)

    def fellow(e):
        return lax.rem(group + e, m)

    barrier = pltpu.get_barrier_semaphore()

    def greet(d, carry):
        pl.semaphore_signal(barrier, inc=1, device_id={"sta": peer(d), "tpl": group}, device_id_type=MESH)
        return carry

    lax.fori_loop(1, n, greet, 0)
    for e in range(1, m):
        pl.semaphore_signal(barrier, inc=1, device_id={"sta": me, "tpl": fellow(e)}, device_id_type=MESH)
    pl.semaphore_wait(barrier, n + m - 2)

    def copy1(d):
        rows = pl.ds(pl.multiple_of(peer(d) * chunk, 8), chunk)
        return pltpu.make_async_remote_copy(
            src_ref=moved_ref.at[rows],
            dst_ref=recv1.at[d],
            send_sem=send1_sem.at[d],
            recv_sem=recv1_sem.at[d],
            device_id={"sta": peer(d), "tpl": group},
            device_id_type=MESH,
        )

    def copy2(d):
        return pltpu.make_async_remote_copy(
            src_ref=send2.at[peer(d)],
            dst_ref=recv2.at[me],
            send_sem=send2_sem.at[d],
            recv_sem=recv2_sem.at[d],
            device_id={"sta": peer(d), "tpl": group},
            device_id_type=MESH,
        )

    def copy3(e):
        return pltpu.make_async_remote_copy(
            src_ref=best,
            dst_ref=bests.at[e],
            send_sem=send3_sem.at[e],
            recv_sem=recv3_sem.at[e],
            device_id={"sta": me, "tpl": fellow(e)},
            device_id_type=MESH,
        )

    def start1(d, carry):
        copy1(d).start()
        return carry

    lax.fori_loop(1, n, start1, 0)

    def gather1(d, acc):
        copy1(d).wait_recv()
        return acc + recv1[d]

    stack = lax.fori_loop(1, n, gather1, moved_ref[pl.ds(pl.multiple_of(me * chunk, 8), chunk), :])
    scales = deviation_scale(stack, groups, n * own)
    scored[chunk:, :] = jnp.zeros((8, LANES), jnp.float32)
    for t in range(groups):
        scored[t * count : (t + 1) * count, :] = stack[t * count : (t + 1) * count, :] / scales[t]
    scale = jnp.concatenate(scales, axis=0)
    lane = lax.broadcasted_iota(jnp.int32, (groups, LANES), 1)
    for j in range(n):
        begin, rest = divmod(own * j, LANES)
        near = scored[pl.ds(begin, groups, stride=count), :]
        if rest:
            after = scored[pl.ds(begin + 1, groups, stride=count), :]
            near = pltpu.roll(jnp.where(lane >= rest, near, after), LANES - rest, 1)
        send2[j] = jnp.where(lane < own, near, scale)

    def start2(d, carry):
        copy2(d).start()
        return carry

    lax.fori_loop(1, n, start2, 0)
    recv2[me] = send2[me]

    def wait2(d, carry):
        copy2(d).wait_recv()
        return carry

    lax.fori_loop(1, n, wait2, 0)
    for i in range(n):
        grid[i * groups : (i + 1) * groups, :] = recv2[i]
    whole = grid[...]
    top = jnp.max(whole, axis=0, keepdims=True)
    best[...] = jnp.broadcast_to(top, best.shape)
    for e in range(1, m):
        copy3(e).start()
    turned = whole.T
    score_ref[...] = turned[:own, :]
    scale_ref[...] = turned[own : own + 1, :]
    for e in range(1, m):
        copy3(e).wait_recv()
        top = jnp.maximum(top, bests[e][:1])
    peak_ref[...] = top[:, :own]

    def finish(d, carry):
        copy1(d).wait_send()
        copy2(d).wait_send()
        return carry

    lax.fori_loop(1, n, finish, 0)
    for e in range(1, m):
        copy3(e).wait_send()


def exchange(moved, rows, n, m):
    chunk = moved.shape[0] // n
    groups = rows // n
    return pl.pallas_call(
        functools.partial(exchange_kernel, n, m),
        out_shape=(
            jax.ShapeDtypeStruct((TOUT_DEV, rows), jnp.float32),
            jax.ShapeDtypeStruct((1, rows), jnp.float32),
            jax.ShapeDtypeStruct((1, TOUT_DEV), jnp.float32),
        ),
        in_specs=[pl.BlockSpec(memory_space=pltpu.VMEM)],
        out_specs=(pl.BlockSpec(memory_space=pltpu.VMEM),) * 3,
        scratch_shapes=[
            pltpu.VMEM((n, chunk, LANES), jnp.float32),
            pltpu.VMEM((chunk + 8, LANES), jnp.float32),
            pltpu.VMEM((n, groups, LANES), jnp.float32),
            pltpu.VMEM((n, groups, LANES), jnp.float32),
            pltpu.VMEM((rows, LANES), jnp.float32),
            pltpu.VMEM((8, LANES), jnp.float32),
            pltpu.VMEM((m, 8, LANES), jnp.float32),
            pltpu.SemaphoreType.DMA((n,)),
            pltpu.SemaphoreType.DMA((n,)),
            pltpu.SemaphoreType.DMA((n,)),
            pltpu.SemaphoreType.DMA((n,)),
            pltpu.SemaphoreType.DMA((m,)),
            pltpu.SemaphoreType.DMA((m,)),
        ],
        compiler_params=pltpu.CompilerParams(collective_id=0, has_side_effects=True),
    )(moved)


def on_device(waveform, templates, lags, present):
    n, m = lax.axis_size("sta"), lax.axis_size("tpl")
    rows = templates.shape[0]
    moved = correlate(waveform[0], templates[:, 0, :], lags[:, 0], present, TOUT_DEV * n)
    score, scale_mad, peak = exchange(moved, rows, n, m)
    return (score, scale_mad[0], peak[0])


def solution(mesh):
    placed = (P("sta", None, None), P("tpl", "sta", None), P("tpl", "sta"), P("tpl", "sta"))
    return jax.shard_map(
        on_device,
        mesh=mesh,
        in_specs=placed,
        out_specs=(P("sta", "tpl"), P("tpl"), P("sta")),
        check_vma=False,
    )
```

time: 600 us -> 32.7 us (0.05); the launches traced: 590 us -> 32.4 us
  local copies, waits for them, and re-layouts: 406 us -> 3.88 us
  waiting for transfers between devices: 96.7 us -> 0 us
  other arithmetic: 54.5 us -> 0 us
  Pallas kernels: 0 us -> 27.9 us
  between operations: 14.2 us -> 0.66 us
  starting transfers between devices: 7.43 us -> 0 us
    gather x257 -> x0, local copies, waits for them, and re-layouts: 262 us -> none
    psum x1 -> x0, waiting for transfers between devices: 87.8 us -> none  [on_device(): summed = lax.psum(counts, 'sta')]
    while x20 -> x0, local copies, waits for them, and re-layouts: 68.7 us -> none
    reshape x6 -> x0, local copies, waits for them, and re-layouts: 46.3 us -> none  [the longest x4 45.5 us: toeplitz_rows(): tiled = tiled.reshape(chans, length, count + 1)[:, :, :columns]]
    add x3 -> x0, other arithmetic: 32.7 us -> none  [the longest x1 32.6 us: hat_counts(): counts + jax.ops.segment_sum(flat_weight, flat_index + 1, num_segments=nc...]
    pallas_call x0 -> x2, Pallas kernels: none -> 27.9 us  [the longest x1 22.7 us: exchange(): pl.pallas_call(functools.partial(exchange_kernel, n, m), out_shape=(jax.S...]
    slice x12 -> x0, local copies, waits for them, and re-layouts: 23.4 us -> none  [the longest x4 15.5 us: toeplitz_rows(): tiled = tiled.reshape(chans, (length + 1) * count)[:, :length * (count + 1)]]
    another operation x4 -> x0, other arithmetic: 18.2 us -> none
  transfers between devices with their start and end apart: 2 -> 0, of which waited for: 2 -> 0; matrix products, arithmetic and copies ran while one was open for 0% -> 0% of each run, Pallas kernels for 0% -> 0%
where the time goes in v1:
time: 32.7 us; the launch traced here: 32.4 us
  Pallas kernels  27.9 us (85%)
  local copies, waits for them, and re-layouts  3.88 us (12%)
  between operations  0.66 us (2%)
    pallas_call x1, Pallas kernels, exchange(): pl.pallas_call(functools.partial(exchange_kernel, n, m), out_shape=(jax.S...  22.7 us
    pallas_call x1, Pallas kernels, correlate(): pl.pallas_call(functools.partial(correlate_kernel, blocks, stride), out_s...  5.15 us
    unnamed x10, local copies, waits for them, and re-layouts  3.88 us

profile of v1, /device:TPU:0, one launch (start us, length us, event | category | flops | bytes accessed | tf_op | source)
XLA Modules:
  0.0 32.4 jit_solution(16722728710063892324)
XLA Ops:
  0.6 0.0 copy-start
  0.6 0.6 %copy-done = s32[64,1]{0,1:T(1,128)S(1)} copy-done((s32[64,1]{0,1:T(1,128)S(1)}, s32[64,1]{0,1:T(1,128)}, u32[]{:S(2)}) %copy-start) | copy-done | bytes 280
  1.3 0.7 %copy.7.present_ref = s32[64,1]{1,0:T(8,128)} copy(s32[64,1]{0,1:T(1,128)S(1)} %copy-done) | data formatting | bytes 512 | tf_op args[3]
  2.0 5.2 %shard_map.67.moved_ref = f32[384,128]{1,0:T(8,128)} custom-call(s32[64]{0:T(128)} %bitcast.7, bf16[3,4279]{1,0:T(4,128)(2,1)} %bitcast.6, bf16[64,1536]{1,0:T(8,128)(2,1)} %bitcast.5, s32[64,1]{1,0:T(8,128)} %copy.7.present_ref), custom_call_target="tpu_custom_call" | custom-call | tf_op jit(solution)/shard_map/pallas_call | solution.py:74
  7.1 22.7 %shard_map.68 = (f32[48,64]{1,0:T(8,128)}, f32[1,64]{1,0:T(1,128)}, f32[1,48]{1,0:T(1,128)}) custom-call(f32[384,128]{1,0:T(8,128)} %shard_map.67.moved_ref), custom_call_target="tpu_custom_call" | custom-call | tf_op jit(solution)/shard_map/pallas_call | solution.py:253
  29.9 0.0 copy-start.2
  29.9 1.3 %copy.11 = f32[48,64]{1,0:T(8,128)} copy(f32[48,64]{1,0:T(8,128)} %get-tuple-element.12) | data formatting | bytes 24576
  31.2 0.0 copy-done.2
  31.2 0.0 copy-start.1
  31.2 0.5 %copy.12 = f32[64]{0:T(128)} copy(f32[64]{0:T(128)S(1)} %bitcast.9) | data formatting | bytes 512
  31.7 0.2 copy-done.1
  31.9 0.5 %copy.13 = f32[48]{0:T(128)} copy(f32[48]{0:T(128)S(1)} %bitcast.8) | data formatting | bytes 384
Async XLA Ops:
  0.6 0.7 %copy-start = (s32[64,1]{0,1:T(1,128)S(1)}, s32[64,1]{0,1:T(1,128)}, u32[]{:S(2)}) copy-start(s32[64,1]{0,1:T(1,128)} %param.7) | copy-start | bytes 772
  29.9 1.4 %copy-start.2 = (f32[1,64]{1,0:T(1,128)S(1)}, f32[1,64]{1,0:T(1,128)}, u32[]{:S(2)}) copy-start(f32[1,64]{1,0:T(1,128)} %get-tuple-element.7) | copy-start | bytes 772
  31.2 0.7 %copy-start.1 = (f32[1,48]{1,0:T(1,128)S(1)}, f32[1,48]{1,0:T(1,128)}, u32[]{:S(2)}) copy-start(f32[1,48]{1,0:T(1,128)} %get-tuple-element.8) | copy-start | bytes 580

commit v2 on v1

v2 whole, which is shorter than its diff:
```python
import functools

import jax
import jax.numpy as jnp
from jax import lax
from jax.experimental import pallas as pl
from jax.experimental.pallas import tpu as pltpu
from jax.sharding import PartitionSpec as P

LEN = 512
LAG = 3000
BINS = 1024
TOUT_DEV = 48
LANES = 128
MESH = pl.DeviceIdType.MESH


def ceil_to(value, step):
    return -(-value // step) * step


def build_hankel(wave_ref, record, hankel):
    chans, samples = wave_ref.shape
    padded = record.shape[1]
    span = hankel.shape[2]
    record[...] = jnp.zeros_like(record)
    record[:, :samples] = wave_ref[...].astype(jnp.float32)
    row = lax.broadcasted_iota(jnp.int32, (8, padded), 0)
    for c in range(chans):
        base = jnp.broadcast_to(record[c : c + 1, :], (8, padded))
        for bit in (1, 2, 4):
            base = jnp.where((row & bit) != 0, pltpu.roll(base, padded - bit, 1), base)
        for g in range(LANES // 16):
            low = pltpu.roll(base, padded - 16 * g, 1) if g else base
            high = pltpu.roll(base, padded - 16 * g - 8, 1)
            both = jnp.concatenate([low[:, :span], high[:, :span]], axis=0)
            hankel[c, 16 * g : 16 * g + 16, :] = both.astype(jnp.bfloat16)


def correlate_blocks(blocks, stride, pattern_ref, hankel, corr):
    chans = hankel.shape[0]
    rows = pattern_ref.shape[0]
    pattern = pattern_ref[...]
    wide = pattern.astype(jnp.float32)
    factor = 1.0 / jnp.sqrt(jnp.sum(wide * wide, axis=1, keepdims=True) + 1e-06)
    for b in range(blocks):
        parts = []
        for c in range(chans):
            for q in range(LEN // LANES):
                begin = 2 * LANES * b + LANES * q
                parts.append(hankel[c, :, begin : begin + 2 * LANES])
        columns = jnp.concatenate(parts, axis=0)
        result = jnp.dot(pattern, columns, preferred_element_type=jnp.float32) * factor
        corr[pl.ds(2 * b, rows, stride=stride), :] = result[:, :LANES]
        corr[pl.ds(2 * b + 1, rows, stride=stride), :] = result[:, LANES:]


def deviation_scale(stack, groups, total):
    width = 512.0 / BINS
    count = stack.shape[0] // groups
    position = jnp.clip(jnp.abs(stack) / width - 0.5, 0.0, BINS - 1.0)
    lower = jnp.minimum(jnp.floor(position), BINS - 2.0)
    coarse = jnp.floor(lower * 0.125)
    fine = position - 8.0 * coarse
    sub = lax.broadcasted_iota(jnp.int32, (LANES, LANES), 0).astype(jnp.float32)
    few = lax.broadcasted_iota(jnp.int32, (16, LANES), 0).astype(jnp.float32)
    tables = []
    for t in range(groups):
        hots, weights = [], []
        for a in range(count):
            r = t * count + a
            hots.append((coarse[r : r + 1, :] == sub).astype(jnp.float32).astype(jnp.bfloat16))
            hat = jnp.maximum(1.0 - jnp.abs(fine[r : r + 1, :] - few), 0.0)
            first = hat.astype(jnp.bfloat16)
            left = hat - first.astype(jnp.float32)
            second = left.astype(jnp.bfloat16)
            third = (left - second.astype(jnp.float32)).astype(jnp.bfloat16)
            weights.append(jnp.concatenate([first, second, third], axis=0))
        hot = jnp.concatenate(hots, axis=1)
        weight = jnp.concatenate(weights, axis=1)
        found = lax.dot_general(weight, hot, (((1,), (1,)), ((), ())), preferred_element_type=jnp.float32)
        found = found[:16] + found[16:32] + found[32:48]
        tables.append(found[:8] + pltpu.roll(found[8:], 1, 1))
    counts = jnp.concatenate(tables, axis=0)
    row = lax.broadcasted_iota(jnp.int32, counts.shape, 0) & 7
    running = counts
    for step in (1, 2, 4):
        running = running + jnp.where(row >= step, pltpu.roll(running, step, 0), 0.0)
    sums = [jnp.broadcast_to(jnp.sum(t, axis=0, keepdims=True), (8, LANES)) for t in tables]
    sums = jnp.concatenate(sums, axis=0)
    upper = (
        lax.broadcasted_iota(jnp.int32, (LANES, LANES), 0) < lax.broadcasted_iota(jnp.int32, (LANES, LANES), 1)
    ).astype(jnp.float32)
    prior = jnp.dot(sums, upper, precision=lax.Precision.HIGHEST, preferred_element_type=jnp.float32)
    earlier = prior + (running - counts)
    share = jnp.clip((0.5 * total - earlier) / jnp.maximum(counts, 1.0), 0.0, 1.0)
    scales = []
    for t in range(groups):
        part = jnp.sum(share[8 * t : 8 * t + 8], axis=0, keepdims=True)
        scales.append(1.4826 * (width * jnp.sum(part, axis=1, keepdims=True)))
    return scales


def stack_kernel(n, m, own, blocks, stride, lags_ref, present_ref, wave_ref, pattern_ref, out_ref, record, hankel, corr, moved, recv1, scored, send2, recv2, send3, recv3, send1_sem, recv1_sem, send2_sem, recv2_sem, send3_sem, recv3_sem):
    me, group = lax.axis_index("sta"), lax.axis_index("tpl")
    groups = send2.shape[1]
    chunk = moved.shape[1]
    count = chunk // groups
    rows = n * groups

    def peer(d):
        return lax.rem(me + d, n)

    def fellow(e):
        return lax.rem(group + e, m)

    barrier = pltpu.get_barrier_semaphore()
    for e in range(m):

        def greet(d, carry):
            pl.semaphore_signal(barrier, inc=1, device_id={"sta": peer(d), "tpl": fellow(e)}, device_id_type=MESH)
            return carry

        lax.fori_loop(0 if e else 1, n, greet, 0)

    def copy1(d):
        return pltpu.make_async_remote_copy(
            src_ref=moved.at[d],
            dst_ref=recv1.at[d],
            send_sem=send1_sem.at[d],
            recv_sem=recv1_sem.at[d],
            device_id={"sta": peer(d), "tpl": group},
            device_id_type=MESH,
        )

    def copy2(d):
        return pltpu.make_async_remote_copy(
            src_ref=send2.at[peer(d)],
            dst_ref=recv2.at[me],
            send_sem=send2_sem.at[d],
            recv_sem=recv2_sem.at[d],
            device_id={"sta": peer(d), "tpl": group},
            device_id_type=MESH,
        )

    def copy3(e, d):
        return pltpu.make_async_remote_copy(
            src_ref=send3.at[peer(d)],
            dst_ref=recv3.at[e, d],
            send_sem=send3_sem.at[e, d],
            recv_sem=recv3_sem.at[e, d],
            device_id={"sta": peer(d), "tpl": fellow(e)},
            device_id_type=MESH,
        )

    build_hankel(wave_ref, record, hankel)
    correlate_blocks(blocks, stride, pattern_ref, hankel, corr)

    lane = lax.broadcasted_iota(jnp.int32, (count, LANES), 1)

    def shift(d):
        for k in range(groups):
            t = peer(d) * groups + k
            lag = lags_ref[t]
            begin = t * stride + (lag >> 7)
            rest = lag & (LANES - 1)
            near = corr[pl.ds(begin, count), :]
            after = corr[pl.ds(begin + 1, count), :]
            joined = pltpu.roll(jnp.where(lane >= rest, near, after), (LANES - rest) & (LANES - 1), 1)
            moved[d, k * count : (k + 1) * count, :] = joined * present_ref[t].astype(jnp.float32)

    batch = max(n // 4, 1)
    for begin in range(1, n, batch):
        for d in range(begin, min(begin + batch, n)):
            shift(d)
        if begin == 1:
            pl.semaphore_wait(barrier, n * m - 1)
        for d in range(begin, min(begin + batch, n)):
            copy1(d).start()
    shift(0)

    def gather1(d, acc):
        copy1(d).wait_recv()
        return acc + recv1[d]

    stack = lax.fori_loop(1, n, gather1, moved[0])
    scales = deviation_scale(stack, groups, n * own)
    scored[chunk:, :] = jnp.zeros((8, LANES), jnp.float32)
    for t in range(groups):
        scored[t * count : (t + 1) * count, :] = stack[t * count : (t + 1) * count, :] / scales[t]
    scale = jnp.concatenate(scales, axis=0)
    lane = lax.broadcasted_iota(jnp.int32, (groups, LANES), 1)
    for j in range(n):
        begin, rest = divmod(own * j, LANES)
        near = scored[pl.ds(begin, groups, stride=count), :]
        if rest:
            after = scored[pl.ds(begin + 1, groups, stride=count), :]
            near = pltpu.roll(jnp.where(lane >= rest, near, after), LANES - rest, 1)
        send2[j] = jnp.where(lane < own, near, scale)
        send3[j] = jnp.max(near, axis=0, keepdims=True)

    def start2(d, carry):
        copy2(d).start()
        return carry

    lax.fori_loop(1, n, start2, 0)
    for e in range(1, m):

        def start3(d, carry):
            copy3(e, d).start()
            return carry

        lax.fori_loop(0, n, start3, 0)
    recv2[me] = send2[me]

    def wait2(d, carry):
        copy2(d).wait_recv()
        return carry

    lax.fori_loop(1, n, wait2, 0)
    top = recv2[0]
    out_ref[:groups, :] = top
    for i in range(1, n):
        out_ref[i * groups : (i + 1) * groups, :] = recv2[i]
        top = jnp.maximum(top, recv2[i])
    top = jnp.max(top, axis=0, keepdims=True)
    for e in range(1, m):

        def wait3(d, best):
            copy3(e, d).wait_recv()
            return jnp.maximum(best, recv3[e, d])

        top = lax.fori_loop(0, n, wait3, top)
    out_ref[rows:, :] = jnp.broadcast_to(top, (8, LANES))

    def finish(d, carry):
        copy1(d).wait_send()
        copy2(d).wait_send()
        return carry

    lax.fori_loop(1, n, finish, 0)
    for e in range(1, m):

        def finish3(d, carry):
            copy3(e, d).wait_send()
            return carry

        lax.fori_loop(0, n, finish3, 0)


def stack_and_score(wave, pattern, lags, present, n, m):
    chans, samples = wave.shape
    rows = pattern.shape[0]
    total = TOUT_DEV * n
    blocks = -(-(total + LAG) // (2 * LANES))
    span = 2 * LANES * blocks + LEN - LANES
    padded = span + LANES
    count = total // LANES
    stride = max(2 * blocks, LAG // LANES + count + 2) | 1
    groups = rows // n
    chunk = groups * count
    smem, vmem = pl.BlockSpec(memory_space=pltpu.SMEM), pl.BlockSpec(memory_space=pltpu.VMEM)
    return pl.pallas_call(
        functools.partial(stack_kernel, n, m, TOUT_DEV, blocks, stride),
        out_shape=jax.ShapeDtypeStruct((rows + 8, LANES), jnp.float32),
        in_specs=[smem, smem, vmem, vmem],
        out_specs=vmem,
        scratch_shapes=[
            pltpu.VMEM((chans, padded), jnp.float32),
            pltpu.VMEM((chans, LANES, span), jnp.bfloat16),
            pltpu.VMEM((rows * stride, LANES), jnp.float32),
            pltpu.VMEM((n, chunk, LANES), jnp.float32),
            pltpu.VMEM((n, chunk, LANES), jnp.float32),
            pltpu.VMEM((chunk + 8, LANES), jnp.float32),
            pltpu.VMEM((n, groups, LANES), jnp.float32),
            pltpu.VMEM((n, groups, LANES), jnp.float32),
            pltpu.VMEM((n, 1, LANES), jnp.float32),
            pltpu.VMEM((m, n, 1, LANES), jnp.float32),
            pltpu.SemaphoreType.DMA((n,)),
            pltpu.SemaphoreType.DMA((n,)),
            pltpu.SemaphoreType.DMA((n,)),
            pltpu.SemaphoreType.DMA((n,)),
            pltpu.SemaphoreType.DMA((m, n)),
            pltpu.SemaphoreType.DMA((m, n)),
        ],
        compiler_params=pltpu.CompilerParams(collective_id=0, has_side_effects=True),
    )(lags, present, wave, pattern)


def finish_kernel(grid_ref, score_ref, scale_ref, peak_ref):
    own, rows = score_ref.shape
    turned = grid_ref[:rows, :].T
    score_ref[...] = turned[:own, :]
    scale_ref[...] = turned[own, :]
    peak_ref[...] = grid_ref[rows, :own]


def on_device(waveform, templates, lags, present):
    n, m = lax.axis_size("sta"), lax.axis_size("tpl")
    rows = templates.shape[0]
    grid = stack_and_score(waveform[0], templates[:, 0, :], lags[:, 0], present[:, 0], n, m)
    return pl.pallas_call(
        finish_kernel,
        out_shape=(
            jax.ShapeDtypeStruct((TOUT_DEV, rows), jnp.float32),
            jax.ShapeDtypeStruct((rows,), jnp.float32),
            jax.ShapeDtypeStruct((TOUT_DEV,), jnp.float32),
        ),
    )(grid)


def solution(mesh):
    placed = (P("sta", None, None), P("tpl", "sta", None), P("tpl", "sta"), P("tpl", "sta"))
    return jax.shard_map(
        on_device,
        mesh=mesh,
        in_specs=placed,
        out_specs=(P("sta", "tpl"), P("tpl"), P("sta")),
        check_vma=False,
    )
```

time: 32.7 us -> 24.8 us (0.76)
  Pallas kernels: 27.9 us -> 23.9 us
  local copies, waits for them, and re-layouts: 3.88 us -> 0 us
    pallas_call x2, Pallas kernels: 27.9 us -> 23.9 us  [the longest x1 22.5 us: stack_and_score(): pl.pallas_call(functools.partial(stack_kernel, n, m, TOUT_DEV, blocks, st...]
    unnamed x10 -> x0, local copies, waits for them, and re-layouts: 3.88 us -> none
where the time goes in v2:
time: 24.8 us; the launch traced here: 24.6 us
  Pallas kernels  23.9 us (96%)
  between operations  0.64 us (3%)
    pallas_call x1, Pallas kernels, stack_and_score(): pl.pallas_call(functools.partial(stack_kernel, n, m, TOUT_DEV, blocks, st...  22.5 us
    pallas_call x1, Pallas kernels, on_device(): pl.pallas_call(finish_kernel, out_shape=(jax.ShapeDtypeStruct((TOUT_DEV,...  1.46 us

profile of v2, /device:TPU:0, one launch (start us, length us, event | category | flops | bytes accessed | tf_op | source)
XLA Modules:
  0.0 24.6 jit_solution(4248601172110998320)
XLA Ops:
  0.6 22.5 %shard_map.67.grid_ref = f32[72,128]{1,0:T(8,128)} custom-call(s32[64]{0:T(128)} %bitcast.6, s32[64]{0:T(128)} %bitcast.7, bf16[3,4279]{1,0:T(4,128)(2,1)} %bitcast.5, bf16[64,1536]{1,0:T(8,128)(2,1)} %bitcast.4), custom_call_target="tpu_custom_call" | custom-call | tf_op jit(solution)/shard_map/pallas_call | solution.py:263
  23.1 1.5 %shard_map.68 = (f32[48,64]{1,0:T(8,128)}, f32[64]{0:T(128)}, f32[48]{0:T(128)}) custom-call(f32[72,128]{1,0:T(8,128)} %shard_map.67.grid_ref), custom_call_target="tpu_custom_call" | custom-call | tf_op jit(solution)/shard_map/pallas_call | solution.py:302

commit v3 on v2

--- a/solution.py
+++ b/solution.py
@@ -25,16 +25,20 @@
     span = hankel.shape[2]
     record[...] = jnp.zeros_like(record)
     record[:, :samples] = wave_ref[...].astype(jnp.float32)
-    row = lax.broadcasted_iota(jnp.int32, (8, padded), 0)
+    piece = span
     for c in range(chans):
-        base = jnp.broadcast_to(record[c : c + 1, :], (8, padded))
-        for bit in (1, 2, 4):
-            base = jnp.where((row & bit) != 0, pltpu.roll(base, padded - bit, 1), base)
-        for g in range(LANES // 16):
-            low = pltpu.roll(base, padded - 16 * g, 1) if g else base
-            high = pltpu.roll(base, padded - 16 * g - 8, 1)
-            both = jnp.concatenate([low[:, :span], high[:, :span]], axis=0)
-            hankel[c, 16 * g : 16 * g + 16, :] = both.astype(jnp.bfloat16)
+        for start in range(0, span, piece):
+            size = min(piece, span - start)
+            wide = size + LANES
+            row = lax.broadcasted_iota(jnp.int32, (8, wide), 0)
+            base = jnp.broadcast_to(record[c : c + 1, start : start + wide], (8, wide))
+            for bit in (1, 2, 4):
+                base = jnp.where((row & bit) != 0, pltpu.roll(base, wide - bit, 1), base)
+            for g in range(LANES // 16):
+                low = pltpu.roll(base, wide - 16 * g, 1) if g else base
+                high = pltpu.roll(base, wide - 16 * g - 8, 1)
+                both = jnp.concatenate([low[:, :size], high[:, :size]], axis=0)
+                hankel[c, 16 * g : 16 * g + 16, start : start + size] = both.astype(jnp.bfloat16)
 
 
 def correlate_blocks(blocks, stride, pattern_ref, hankel, corr):
@@ -101,7 +105,7 @@
     return scales
 
 
-def stack_kernel(n, m, own, blocks, stride, lags_ref, present_ref, wave_ref, pattern_ref, out_ref, record, hankel, corr, moved, recv1, scored, send2, recv2, send3, recv3, send1_sem, recv1_sem, send2_sem, recv2_sem, send3_sem, recv3_sem):
+def stack_kernel(n, m, own, blocks, stride, lags_hbm, present_hbm, wave_hbm, pattern_hbm, out_ref, lags_ref, present_ref, wave_ref, pattern_ref, load_sem, record, hankel, corr, moved, recv1, scored, send2, recv2, send3, recv3, send1_sem, recv1_sem, send2_sem, recv2_sem, send3_sem, recv3_sem):
     me, group = lax.axis_index("sta"), lax.axis_index("tpl")
     groups = send2.shape[1]
     chunk = moved.shape[1]
@@ -113,6 +117,15 @@
 
     def fellow(e):
         return lax.rem(group + e, m)
+
+    loads = [
+        pltpu.make_async_copy(source, target, load_sem.at[k])
+        for k, (source, target) in enumerate(
+            ((wave_hbm, wave_ref), (pattern_hbm, pattern_ref), (lags_hbm, lags_ref), (present_hbm, present_ref))
+        )
+    ]
+    for load in loads:
+        load.start()
 
     barrier = pltpu.get_barrier_semaphore()
     for e in range(m):
@@ -153,9 +166,13 @@
             device_id_type=MESH,
         )
 
+    loads[0].wait()
     build_hankel(wave_ref, record, hankel)
+    loads[1].wait()
     correlate_blocks(blocks, stride, pattern_ref, hankel, corr)
 
+    loads[2].wait()
+    loads[3].wait()
     lane = lax.broadcasted_iota(jnp.int32, (count, LANES), 1)
 
     def shift(d):
@@ -169,13 +186,14 @@
             joined = pltpu.roll(jnp.where(lane >= rest, near, after), (LANES - rest) & (LANES - 1), 1)
             moved[d, k * count : (k + 1) * count, :] = joined * present_ref[t].astype(jnp.float32)
 
+    far_first = sorted(range(1, n), key=lambda d: abs(d - n // 2))
     batch = max(n // 4, 1)
-    for begin in range(1, n, batch):
-        for d in range(begin, min(begin + batch, n)):
+    for begin in range(0, n - 1, batch):
+        for d in far_first[begin : begin + batch]:
             shift(d)
-        if begin == 1:
+        if begin == 0:
             pl.semaphore_wait(barrier, n * m - 1)
-        for d in range(begin, min(begin + batch, n)):
+        for d in far_first[begin : begin + batch]:
             copy1(d).start()
     shift(0)
 
@@ -199,18 +217,18 @@
         send2[j] = jnp.where(lane < own, near, scale)
         send3[j] = jnp.max(near, axis=0, keepdims=True)
 
+    for e in range(1, m):
+
+        def start3(d, carry):
+            copy3(e, d).start()
+            return carry
+
+        lax.fori_loop(0, n, start3, 0)
     def start2(d, carry):
         copy2(d).start()
         return carry
 
     lax.fori_loop(1, n, start2, 0)
-    for e in range(1, m):
-
-        def start3(d, carry):
-            copy3(e, d).start()
-            return carry
-
-        lax.fori_loop(0, n, start3, 0)
     recv2[me] = send2[me]
 
     def wait2(d, carry):
@@ -231,7 +249,9 @@
             return jnp.maximum(best, recv3[e, d])
 
         top = lax.fori_loop(0, n, wait3, top)
-    out_ref[rows:, :] = jnp.broadcast_to(top, (8, LANES))
+    lane = lax.broadcasted_iota(jnp.int32, (8, LANES), 1)
+    moved_top = jnp.broadcast_to(pltpu.roll(top, LANES // 2, 1), (8, LANES))
+    out_ref[:8, :] = jnp.where(lane < LANES // 2, out_ref[:8, :], moved_top)
 
     def finish(d, carry):
         copy1(d).wait_send()
@@ -259,13 +279,18 @@
     stride = max(2 * blocks, LAG // LANES + count + 2) | 1
     groups = rows // n
     chunk = groups * count
-    smem, vmem = pl.BlockSpec(memory_space=pltpu.SMEM), pl.BlockSpec(memory_space=pltpu.VMEM)
+    vmem = pl.BlockSpec(memory_space=pltpu.VMEM)
     return pl.pallas_call(
         functools.partial(stack_kernel, n, m, TOUT_DEV, blocks, stride),
-        out_shape=jax.ShapeDtypeStruct((rows + 8, LANES), jnp.float32),
-        in_specs=[smem, smem, vmem, vmem],
+        out_shape=jax.ShapeDtypeStruct((rows, LANES), jnp.float32),
+        in_specs=[pl.BlockSpec(memory_space=pl.ANY)] * 4,
         out_specs=vmem,
         scratch_shapes=[
+            pltpu.SMEM(lags.shape, lags.dtype),
+            pltpu.SMEM(present.shape, present.dtype),
+            pltpu.VMEM(wave.shape, wave.dtype),
+            pltpu.VMEM(pattern.shape, pattern.dtype),
+            pltpu.SemaphoreType.DMA((4,)),
             pltpu.VMEM((chans, padded), jnp.float32),
             pltpu.VMEM((chans, LANES, span), jnp.bfloat16),
             pltpu.VMEM((rows * stride, LANES), jnp.float32),
@@ -289,10 +314,10 @@
 
 def finish_kernel(grid_ref, score_ref, scale_ref, peak_ref):
     own, rows = score_ref.shape
-    turned = grid_ref[:rows, :].T
+    turned = grid_ref[...].T
     score_ref[...] = turned[:own, :]
     scale_ref[...] = turned[own, :]
-    peak_ref[...] = grid_ref[rows, :own]
+    peak_ref[...] = grid_ref[0, LANES // 2 : LANES // 2 + own]
 
 
 def on_device(waveform, templates, lags, present):

time: 24.8 us -> 23.4 us (0.944)
  Pallas kernels: 23.9 us -> 22.6 us
    pallas_call x1, Pallas kernels: 22.5 us -> 21.1 us  [stack_and_score(): pl.pallas_call(functools.partial(stack_kernel, n, m, TOUT_DEV, blocks, st...]
where the time goes in v3:
time: 23.4 us; the launch traced here: 23.2 us
  Pallas kernels  22.6 us (97%)
  between operations  0.64 us (3%)
    pallas_call x1, Pallas kernels, stack_and_score(): pl.pallas_call(functools.partial(stack_kernel, n, m, TOUT_DEV, blocks, st...  21.1 us
    pallas_call x1, Pallas kernels, on_device(): pl.pallas_call(finish_kernel, out_shape=(jax.ShapeDtypeStruct((TOUT_DEV,...  1.47 us

profile of v3, /device:TPU:0, one launch (start us, length us, event | category | flops | bytes accessed | tf_op | source)
XLA Modules:
  0.0 23.2 jit_solution(188294580288461309)
XLA Ops:
  0.6 21.1 %shard_map.67.grid_ref = f32[64,128]{1,0:T(8,128)} custom-call(s32[64]{0:T(128)} %bitcast.6, s32[64]{0:T(128)} %bitcast.7, bf16[3,4279]{1,0:T(4,128)(2,1)} %bitcast.5, bf16[64,1536]{1,0:T(8,128)(2,1)} %bitcast.4), custom_call_target="tpu_custom_call" | custom-call | tf_op jit(solution)/shard_map/pallas_call | solution.py:283
  21.7 1.5 %shard_map.68 = (f32[48,64]{1,0:T(8,128)}, f32[64]{0:T(128)}, f32[48]{0:T(128)}) custom-call(f32[64,128]{1,0:T(8,128)} %shard_map.67.grid_ref), custom_call_target="tpu_custom_call" | custom-call | tf_op jit(solution)/shard_map/pallas_call | solution.py:327
